TPU v7x, 32 devices: a whole 2x2x4 slice. The times are simulated.
32 devices in a mesh: rows: 16 (over z, y, x), cols: 2 (over core).
Axes of the slice: x: 2, y: 2, z: 4, core: 2. Of those that a mesh axis runs over, the one named last changes fastest.
Arguments:
- design: float32 [16384, 512], P('rows', 'cols'), may hold values from -24 to 24
- signs: int32 [16384], P('rows'), may hold values from -1 to 1, as said below
- kept: int32 [1024], replicated, may hold values from 0 to 16383, as said below
Outputs:
- sketch: float32 [1024, 512], P('rows', 'cols')
- factor: float32 [512, 512], P(None, 'cols')
Inputs may be any that keep to these rules, and one draw needn't show every extreme that they name: `signs`: each entry is +1 or -1. `kept`: distinct and increasing.
All inputs are finite; a program needn't handle non-finite values.
Results may differ from a plain program's by a relative error of at most 0.0003.
Values sent between devices are 32-bit elements; how exact they have to be, the bound alone decides.
A program may use at most 64 MiB of HBM per device.

v0:
```python
import math
import jax
import jax.numpy as jnp
from jax import lax
from jax.sharding import PartitionSpec as P


def hadamard(order):
    matrix = jnp.ones((1, 1), jnp.float32)
    base = jnp.array([[1.0, 1.0], [1.0, -1.0]], jnp.float32)
    while matrix.shape[0] < order:
        matrix = jnp.kron(matrix, base)
    return matrix


def bit_parity(value):
    folded = value
    for amount in (16, 8, 4, 2, 1):
        folded = jnp.bitwise_xor(folded, jnp.right_shift(folded, amount))
    return jnp.bitwise_and(folded, 1)


def local_transform(flipped):
    length, width = flipped.shape
    outer = length // 128
    inner_table = hadamard(128)
    outer_table = hadamard(outer)
    blocks = flipped.reshape(outer, 128, width)
    mixed = jnp.einsum("pb,abc->apc", inner_table, blocks, precision=lax.Precision.HIGHEST)
    mixed = jnp.einsum("qa,apc->qpc", outer_table, mixed, precision=lax.Precision.HIGHEST)
    return mixed.reshape(length, width)


def signed_rows(transformed, kept_part, device_row, total_rows):
    length = transformed.shape[0]
    kept_blocks = kept_part // length
    offsets = kept_part - kept_blocks * length
    parity = bit_parity(jnp.bitwise_and(kept_blocks, device_row))
    factor = (1.0 - 2.0 * parity.astype(jnp.float32)) / math.sqrt(total_rows)
    return jnp.take(transformed, offsets, axis=0) * factor[:, None]


def source_total(received):
    return jnp.sum(received, axis=0)


def body(design, signs, kept):
    flipped = design * signs.astype(jnp.float32)[:, None]
    transformed = local_transform(flipped)
    device_row = lax.axis_index("rows")
    groups = lax.axis_size("rows")
    length = transformed.shape[0]
    widths = transformed.shape[1]
    total_rows = length * groups
    per_device = kept.shape[0] // groups
    outgoing = signed_rows(transformed, kept, device_row, total_rows)
    outgoing = outgoing.reshape(groups, per_device, widths)
    sketch = source_total(lax.all_to_all(outgoing, "rows", split_axis=0, concat_axis=0, tiled=True))
    column = lax.axis_index("cols")
    whole = lax.all_gather(sketch, "cols", axis=1, tiled=True)
    kept_total = kept.shape[0]
    partial_gram = jnp.dot(
        whole.T, whole, precision=lax.Precision.HIGHEST, preferred_element_type=jnp.float32
    )
    gram = lax.psum(partial_gram, "rows") / kept_total
    factor = jnp.linalg.cholesky(gram).T
    return (sketch, lax.dynamic_slice_in_dim(factor, column * widths, widths, 1))


def solution(mesh):
    placed = (P("rows", "cols"), P("rows"), P())
    return jax.shard_map(
        body,
        mesh=mesh,
        in_specs=placed,
        out_specs=(P("rows", "cols"), P(None, "cols")),
        check_vma=False,
    )
```

profile of v0, /device:TPU:0, one launch (start us, length us, event | category | flops | bytes accessed | tf_op | source)
XLA Modules:
  0.0 271.5 jit_solution(705625595434788475)
XLA Ops:
  7.2 0.8 broadcast_multiply_fusion.7
  8.0 0.1 mul.252
  8.1 0.8 broadcast_multiply_fusion.6
  8.9 0.1 mul.256
  9.0 0.1 reshape.203
  9.0 0.7 broadcast_clamp_fusion
  9.7 0.7 compare_and_fusion
  10.4 0.8 broadcast_multiply_fusion.5
  11.2 0.1 mul.270
  11.3 0.8 broadcast_multiply_fusion.4
  12.1 0.1 mul.274
  12.2 0.9 broadcast_multiply_fusion.2
  13.1 0.6 mul.278
  13.8 3.1 %broadcast_multiply_fusion = f32[64,2,64,2]{3,2,1,0:T(8,128)} fusion(f32[2,2]{1,0:T(2,128)} %constant.202.clone, f32[64,64]{1,0:T(8,128)S(1)} %mul.278), kind=kLoop, calls=%fused_computation.1 | loop fusion | flops 16384 | bytes 81936 | tf_op jit(solution)/shard_map/jit(kron)/mul | solution.py:12
  16.9 4.0 %reshape.202 = f32[128,128,1]{1,0,2:T(8,128)S(1)} reshape(f32[64,2,64,2]{3,2,1,0:T(8,128)} %broadcast_multiply_fusion) | data formatting | bytes 131072 | tf_op jit(solution)/shard_map/jit(kron)/mul | solution.py:12
  20.9 0.2 broadcast_multiply_fusion.3
  21.1 1.8 fusion.23
  22.9 0.5 copy.14
  23.4 1.0 fusion.1
  24.4 0.3 copy.10
  24.9 0.1 broadcast_in_dim.52
  25.0 3.5 %gather_fusion = f32[1024,256]{1,0:T(8,128)S(1)} fusion(f32[1024,256]{1,0:T(8,128)S(1)} %bitcast.43, s32[1024]{0:T(1024)S(1)} %broadcast_clamp_fusion), kind=kCustom, calls=%fused_computation | custom fusion | bytes 2101248 | tf_op jit(solution)/shard_map/jit(_take)/gather | solution.py:40
  28.4 0.3 select_multiply_fusion
  28.8 34.5 %all_to_all.5 = f32[16,64,256]{2,1,0:T(8,128)S(1)} all-to-all(f32[16,64,256]{2,1,0:T(8,128)S(1)} %select_multiply_fusion), channel_id=1, replica_groups=mesh['rows'=16,'cols'=2] {'rows'}, dimensions={0} | all-to-all | bytes 2097152 | tf_op jit(solution)/shard_map/all_to_all | solution.py:58
  63.3 2.1 all_gather.3
  65.4 2.1 fusion.24
  67.5 110.9 %all-reduce.3.cloned.1.call-done = f32[512,512]{0,1:T(8,128)} async-done(((f32[512,512]{0,1:T(8,128)}), f32[512,512]{0,1:T(8,128)}) %all-reduce.3.cloned.1.call-update) | async-done | bytes 1048592 | tf_op jit(solution)/shard_map/psum | solution.py:65
  178.4 1.4 broadcast_multiply_fusion.1
  179.8 0.3 copy.12
  180.1 0.2 fusion
  180.4 11.7 %cholesky.104 = f32[128,128]{1,0:T(8,128)S(1)} custom-call(f32[128,128]{1,0:T(8,128)S(1)} %cholesky.266), custom_call_target="Cholesky" | custom-call | tf_op jit(solution)/shard_map/jit(cholesky)/cholesky | solution.py:66
  192.1 0.1 cholesky.224
  192.3 9.8 %custom-call.27 = f32[1,128,128]{1,2,0:T(8,128)S(1)} custom-call(f32[1,128,128]{2,1,0:T(8,128)S(1)} %get-tuple-element.15), custom_call_target="InvertDiagBlocksLowerTriangular" | custom-call | tf_op jit(solution)/shard_map/jit(cholesky)/cholesky | solution.py:66
  202.1 0.3 constant_dynamic-update-slice_fusion.1
  202.4 0.3 convolution_subtract_fusion
  202.7 11.7 %cholesky.217 = f32[128,128]{1,0:T(8,128)S(1)} custom-call(f32[128,128]{1,0:T(8,128)S(1)} %cholesky.270), custom_call_target="Cholesky" | custom-call | tf_op jit(solution)/shard_map/jit(cholesky)/cholesky | solution.py:66
  214.5 9.9 %custom-call.28 = f32[1,128,128]{1,2,0:T(8,128)S(1)} custom-call(f32[1,128,128]{2,1,0:T(8,128)S(1)} %get-tuple-element.12), custom_call_target="InvertDiagBlocksLowerTriangular" | custom-call | tf_op jit(solution)/shard_map/jit(cholesky)/cholesky | solution.py:66
  224.4 0.3 convolution_dynamic-update-slice_fusion
  224.7 0.4 convolution_subtract_fusion.1
  225.1 11.7 %cholesky.238 = f32[128,128]{1,0:T(8,128)S(1)} custom-call(f32[128,128]{1,0:T(8,128)S(1)} %cholesky.275), custom_call_target="Cholesky" | custom-call | tf_op jit(solution)/shard_map/jit(cholesky)/cholesky | solution.py:66
  236.8 0.7 compare_reduce_fusion.1
  237.6 9.8 %custom-call.29 = f32[1,128,128]{1,2,0:T(8,128)S(1)} custom-call(f32[1,128,128]{2,1,0:T(8,128)S(1)} %get-tuple-element.9), custom_call_target="InvertDiagBlocksLowerTriangular" | custom-call | tf_op jit(solution)/shard_map/jit(cholesky)/cholesky | solution.py:66
  247.4 0.2 convolution_dynamic-update-slice_fusion.1
  247.6 0.4 convolution_subtract_fusion.2
  248.0 11.7 %cholesky.255 = f32[128,128]{1,0:T(8,128)S(1)} custom-call(f32[128,128]{1,0:T(8,128)S(1)} %convolution_subtract_fusion.2), custom_call_target="Cholesky" | custom-call | tf_op jit(solution)/shard_map/jit(cholesky)/cholesky | solution.py:66
  259.7 0.6 compare_reduce_fusion
  260.4 0.7 compare_reduce_fusion.2
  263.6 1.0 copy.13
  (24 shorter events, 0.5 us)
Async XLA Ops:
  7.2 171.2 %all-reduce.3.cloned.1.call-start = ((), (), s32[]{:S(2)}) async-start(), calls=%async_computation.1 | async-start | bytes 2097152 | tf_op jit(solution)/shard_map/psum | solution.py:65
  13.8 7.1 %copy-start.4 = (s32[1024]{0:T(1024)S(1)}, s32[1024]{0:T(1024)}, u32[]{:S(2)}) copy-start(s32[1024]{0:T(1024)} %param.6) | copy-start | bytes 12292
  13.8 7.1 %copy-start.1 = (f32[1024,256]{1,0:T(8,128)S(1)}, f32[1024,256]{1,0:T(8,128)}, u32[]{:S(2)}) copy-start(f32[1024,256]{1,0:T(8,128)} %param.5) | copy-start | bytes 3145732
  21.1 3.6 %copy-start.3 = (s32[1024]{0:T(1024)S(1)}, s32[1024]{0:T(1024)}, u32[]{:S(2)}) copy-start(s32[1024]{0:T(1024)} %param.7) | copy-start | bytes 12292
  63.3 117.1 %copy-start.2 = (f32[64,256]{1,0:T(8,128)}, f32[64,256]{1,0:T(8,128)S(1)}, u32[]{:S(2)}) copy-start(f32[64,256]{1,0:T(8,128)S(1)} %reduce_sum.9) | copy-start | bytes 196612
  178.3 1.8 copy-start
Sparse Core Ops, SparseCore 0:
  67.6 110.7 all-reduce.2
where the time goes:
time: 272 us; the launch traced here: 271 us
  waiting for transfers between devices  111 us (41%)
  other arithmetic  89.4 us (33%)
  blocking collectives  36.5 us (13%)
  between operations  16.9 us (6%)
  local copies, waits for them, and re-layouts  11 us (4%)
  matrix products  6.7 us (2%)
    psum x1, waiting for transfers between devices, body(): gram = lax.psum(partial_gram, 'rows') / kept_total  111 us
    another operation x14, other arithmetic, body(): factor = jnp.linalg.cholesky(gram).T  78.6 us
    all_to_all x1, blocking collectives, body(): lax.all_to_all(outgoing, 'rows', split_axis=0, concat_axis=0, tiled=True)  34.5 us
    mul x6, other arithmetic, hadamard(): matrix = jnp.kron(matrix, base)  7.1 us
  transfers between devices with their start and end apart: 1, of which 1 were waited for; matrix products, arithmetic and copies ran while one was open for 0% of the time, Pallas kernels for 0%

commit v1 on v0

--- a/solution.py
+++ b/solution.py
@@ -62,7 +62,7 @@
     partial_gram = jnp.dot(
         whole.T, whole, precision=lax.Precision.HIGHEST, preferred_element_type=jnp.float32
     )
-    gram = lax.psum(partial_gram, "rows") / kept_total
+    gram = lax.all_gather(partial_gram, axis_name="rows").sum(axis=0) / kept_total
     factor = jnp.linalg.cholesky(gram).T
     return (sketch, lax.dynamic_slice_in_dim(factor, column * widths, widths, 1))
 

time: 272 us -> 359 us (1.32)
  waiting for transfers between devices: 111 us -> 190 us
  other arithmetic: 89.4 us -> 97.6 us
    all_gather x0 -> x1, waiting for transfers between devices: none -> 189 us  [body(): lax.all_gather(partial_gram, axis_name='rows').sum(axis=0) / kept_total]
    psum x1 -> x0, waiting for transfers between devices: 111 us -> none  [body(): gram = lax.psum(partial_gram, 'rows') / kept_total]
    reduce_sum x0 -> x1, other arithmetic: none -> 7.91 us  [body(): lax.all_gather(partial_gram, axis_name='rows').sum(axis=0) / kept_total]
where the time goes in v1:
time: 359 us; the launch traced here: 358 us
  waiting for transfers between devices  190 us (53%)
  other arithmetic  97.6 us (27%)
  blocking collectives  36.5 us (10%)
  between operations  16.8 us (5%)
  local copies, waits for them, and re-layouts  11 us (3%)
  matrix products  6.67 us (2%)
    all_gather x1, waiting for transfers between devices, body(): lax.all_gather(partial_gram, axis_name='rows').sum(axis=0) / kept_total  189 us
    another operation x14, other arithmetic, body(): factor = jnp.linalg.cholesky(gram).T  78.9 us
    all_to_all x1, blocking collectives, body(): lax.all_to_all(outgoing, 'rows', split_axis=0, concat_axis=0, tiled=True)  34.5 us
    reduce_sum x1, other arithmetic, body(): lax.all_gather(partial_gram, axis_name='rows').sum(axis=0) / kept_total  7.91 us
  transfers between devices with their start and end apart: 1, of which 1 were waited for; matrix products, arithmetic and copies ran while one was open for 0% of the time, Pallas kernels for 0%

profile of v1, /device:TPU:0, one launch (start us, length us, event | category | flops | bytes accessed | tf_op | source)
XLA Modules:
  0.0 358.2 jit_solution(8555973269442215152)
XLA Ops:
  7.2 0.7 compare_and_fusion
  7.9 0.7 broadcast_clamp_fusion
  8.6 0.8 broadcast_multiply_fusion.6
  9.4 0.1 mul.252
  9.5 0.8 broadcast_multiply_fusion.5
  10.3 0.1 reshape.204
  10.5 0.7 fusion.19
  11.3 0.7 convert_element_type.6
  12.0 0.8 broadcast_multiply_fusion.4
  12.8 0.1 mul.270
  12.8 0.8 broadcast_multiply_fusion.3
  13.6 0.1 mul.274
  13.8 0.9 broadcast_multiply_fusion.1
  14.7 0.6 mul.278
  15.3 3.1 broadcast_multiply_fusion
  18.4 4.0 %reshape.203 = f32[128,128,1]{1,0,2:T(8,128)S(1)} reshape(f32[64,2,64,2]{3,2,1,0:T(8,128)} %broadcast_multiply_fusion) | data formatting | bytes 131072 | tf_op jit(solution)/shard_map/jit(kron)/mul | solution.py:12
  22.4 0.2 broadcast_multiply_fusion.2
  22.6 1.8 convolution_bitcast_fusion
  24.5 0.5 copy.13
  24.9 1.0 fusion.21
  25.9 0.3 copy.14
  26.3 3.5 gather_fusion
  29.7 0.3 select_multiply_fusion
  30.1 34.5 %all_to_all.5 = f32[16,64,256]{2,1,0:T(8,128)S(1)} all-to-all(f32[16,64,256]{2,1,0:T(8,128)S(1)} %select_multiply_fusion), channel_id=1, replica_groups=mesh['rows'=16,'cols'=2] {'rows'}, dimensions={0} | all-to-all | bytes 2097152 | tf_op jit(solution)/shard_map/all_to_all | solution.py:58
  64.6 2.1 all_gather.9
  66.7 2.0 fusion.22
  68.7 189.5 %all-gather.3.cloned.1.call-done = f32[8192,512]{1,0:T(8,128)} async-done(((f32[512,512]{1,0:T(8,128)}), f32[8192,512]{1,0:T(8,128)}) %all-gather.3.cloned.1.call-update) | async-done | bytes 16777232 | tf_op jit(solution)/shard_map/all_gather | solution.py:65
  258.2 7.9 %reduce_sum.21 = f32[512,512]{1,0:T(8,128)S(1)} reduce(f32[16,512,512]{2,1,0:T(8,128)} %bitcast.45, f32[]{:T(128)} %constant.195.clone.1), dimensions={0}, to_apply=%region_1.2 | reduce | flops 3932160 | bytes 17825796 | tf_op jit(solution)/shard_map/reduce_sum | solution.py:65
  266.2 0.3 copy.15
  266.5 0.2 fusion
  266.7 11.7 %cholesky.104 = f32[128,128]{1,0:T(8,128)S(1)} custom-call(f32[128,128]{1,0:T(8,128)S(1)} %cholesky.266), custom_call_target="Cholesky" | custom-call | tf_op jit(solution)/shard_map/jit(cholesky)/cholesky | solution.py:66
  278.5 0.1 cholesky.224
  278.6 9.8 %custom-call.27 = f32[1,128,128]{1,2,0:T(8,128)S(1)} custom-call(f32[1,128,128]{2,1,0:T(8,128)S(1)} %get-tuple-element.17), custom_call_target="InvertDiagBlocksLowerTriangular" | custom-call | tf_op jit(solution)/shard_map/jit(cholesky)/cholesky | solution.py:66
  288.4 0.3 constant_dynamic-update-slice_fusion.1
  288.8 0.3 convolution_subtract_fusion
  289.1 11.9 %cholesky.217 = f32[128,128]{1,0:T(8,128)S(1)} custom-call(f32[128,128]{1,0:T(8,128)S(1)} %cholesky.270), custom_call_target="Cholesky" | custom-call | tf_op jit(solution)/shard_map/jit(cholesky)/cholesky | solution.py:66
  301.1 9.8 %custom-call.28 = f32[1,128,128]{1,2,0:T(8,128)S(1)} custom-call(f32[1,128,128]{2,1,0:T(8,128)S(1)} %get-tuple-element.14), custom_call_target="InvertDiagBlocksLowerTriangular" | custom-call | tf_op jit(solution)/shard_map/jit(cholesky)/cholesky | solution.py:66
  310.9 0.3 convolution_dynamic-update-slice_fusion
  311.2 0.4 convolution_subtract_fusion.1
  311.6 11.7 %cholesky.238 = f32[128,128]{1,0:T(8,128)S(1)} custom-call(f32[128,128]{1,0:T(8,128)S(1)} %cholesky.275), custom_call_target="Cholesky" | custom-call | tf_op jit(solution)/shard_map/jit(cholesky)/cholesky | solution.py:66
  323.3 0.7 compare_reduce_fusion.1
  324.0 9.8 %custom-call.29 = f32[1,128,128]{1,2,0:T(8,128)S(1)} custom-call(f32[1,128,128]{2,1,0:T(8,128)S(1)} %get-tuple-element.11), custom_call_target="InvertDiagBlocksLowerTriangular" | custom-call | tf_op jit(solution)/shard_map/jit(cholesky)/cholesky | solution.py:66
  333.8 0.2 convolution_dynamic-update-slice_fusion.1
  334.0 0.4 convolution_subtract_fusion.2
  334.4 12.0 %cholesky.255 = f32[128,128]{1,0:T(8,128)S(1)} custom-call(f32[128,128]{1,0:T(8,128)S(1)} %convolution_subtract_fusion.2), custom_call_target="Cholesky" | custom-call | tf_op jit(solution)/shard_map/jit(cholesky)/cholesky | solution.py:66
  346.4 0.6 compare_reduce_fusion
  347.1 0.7 compare_reduce_fusion.2
  350.4 1.0 copy.16
  (18 shorter events, 0.6 us)
Async XLA Ops:
  7.2 251.1 %all-gather.3.cloned.1.call-start = ((), (), s32[]{:S(2)}) async-start(), calls=%async_computation.1 | async-start | bytes 17825792 | tf_op jit(solution)/shard_map/all_gather | solution.py:65
  15.3 7.1 %copy-start = (f32[1024,256]{1,0:T(8,128)S(1)}, f32[1024,256]{1,0:T(8,128)}, u32[]{:S(2)}) copy-start(f32[1024,256]{1,0:T(8,128)} %param.5) | copy-start | bytes 3145732
  64.6 201.5 %copy-start.1 = (f32[64,256]{1,0:T(8,128)}, f32[64,256]{1,0:T(8,128)S(1)}, u32[]{:S(2)}) copy-start(f32[64,256]{1,0:T(8,128)S(1)} %reduce_sum.20) | copy-start | bytes 196612
Sparse Core Ops, SparseCore 0:
  68.9 189.3 all-gather.2
